TPU v7x, 32 devices: a whole 2x2x4 slice. The times are simulated.
32 devices in a mesh: seq: 8 (over y, x, core), sub: 4 (over z).
Axes of the slice: x: 2, y: 2, z: 4, core: 2. Of those that a mesh axis runs over, the one named last changes fastest.
Arguments:
- tokens: bfloat16 [2048, 4096], P('seq'), may hold values from -6 to 6
- w_split: bfloat16 [4096, 4096], P(None, 'sub'), may hold values from -0.09375 to 0.09375
- w_merge: bfloat16 [4096, 4096], P('sub'), may hold values from -0.09375 to 0.09375
- expert_in: bfloat16 [32, 1024, 2048], P(('seq', 'sub')), may hold values from -0.1875 to 0.1875
- expert_out: bfloat16 [32, 1024, 1024], P(('seq', 'sub')), may hold values from -0.1875 to 0.1875
- expert_ids: int32 [4, 2048, 2], P('sub', 'seq'), may hold values from 0 to 31, all different within a row; in each aligned block of 256 rows (0 to 255, 256 to 511, ..., all dimensions but the last counted through in order) at most 24 rows name the same one
- combine_q: int32 [4, 2048, 2], P('sub', 'seq'), may hold values from 4096 to 65536
- capacity: int32 [32], replicated, may hold values from 12 to 24
Outputs:
- mixed: bfloat16 [2048, 4096], P('seq', 'sub')
Inputs may be any that keep to these rules, and one draw needn't show every extreme that they name: `expert_ids`: in each block of 256 positions of one sub-head, the ids of a position differ, no expert is named more than 24 times, a bound that some block reaches.
All inputs are finite; a program needn't handle non-finite values.
Results may differ from a plain program's by a relative error of at most 0.0076.
Values may be sent and summed in bfloat16 or wider, within the bound.
A program may use at most 128 MiB of HBM per device.

v0:
```python
import jax
import jax.numpy as jnp
from jax import lax
from jax.sharding import PartitionSpec as P


def expert_rows(received, expert_in, expert_out):
    dims_in = received.shape
    rows_flat = received.reshape(-1, dims_in[-1])
    gate_up = jnp.dot(rows_flat, expert_in[0], preferred_element_type=jnp.float32)
    ffe_width = expert_out.shape[1]
    hidden = (jax.nn.silu(gate_up[:, :ffe_width]) * gate_up[:, ffe_width:]).astype(jnp.bfloat16)
    result = jnp.dot(hidden, expert_out[0], preferred_element_type=jnp.float32).astype(jnp.bfloat16)
    return result.reshape(dims_in)


def body(tokens, w_split, w_merge, expert_in, expert_out, expert_ids, combine_q, capacity):
    sub_tok = jnp.dot(tokens, w_split, preferred_element_type=jnp.float32).astype(jnp.bfloat16)
    tok_rows = tokens.shape[0]
    experts = capacity.shape[0]
    slot_count = 3 * tok_rows // experts
    expert_of = expert_ids[0].reshape(-1)
    onehot = (expert_of[:, None] == jnp.arange(experts, dtype=jnp.int32)[None, :]).astype(jnp.int32)
    order_rank = jnp.sum((jnp.cumsum(onehot, axis=0) - onehot) * onehot, axis=1)
    cap_limit = jnp.sum(onehot * capacity[None, :], axis=1)
    is_kept = order_rank < cap_limit
    slot_index = jnp.where(is_kept, expert_of * slot_count + order_rank, -1)
    target = jnp.arange(experts * slot_count, dtype=jnp.int32)
    chosen = jnp.any(
        target[:, None, None] == slot_index.reshape(tok_rows, -1)[None, :, :], axis=2
    ).astype(jnp.bfloat16)
    packed = jnp.dot(chosen, sub_tok, preferred_element_type=jnp.float32).astype(jnp.bfloat16)
    packed = packed.reshape(experts, slot_count, -1)
    answered = expert_rows(
        lax.all_to_all(packed, ("seq", "sub"), split_axis=0, concat_axis=0, tiled=True),
        expert_in,
        expert_out,
    )
    returned_rows = lax.all_to_all(
        answered, ("seq", "sub"), split_axis=0, concat_axis=0, tiled=True
    )
    returned_rows = returned_rows.reshape(experts * slot_count, -1)
    gathered = returned_rows[jnp.maximum(slot_index, 0)].astype(jnp.float32)
    weight = jnp.where(is_kept, combine_q[0].reshape(-1).astype(jnp.float32) / 65536.0, 0.0)
    weighted = (weight[:, None] * gathered).reshape(tok_rows, -1, gathered.shape[1])
    head_out = jnp.sum(weighted, axis=1).astype(jnp.bfloat16)
    partial_value = jnp.dot(head_out, w_merge, preferred_element_type=jnp.float32)
    return lax.psum_scatter(partial_value, "sub", scatter_dimension=1, tiled=True).astype(
        jnp.bfloat16
    )


def solution(mesh):
    in_specs = (
        P("seq", None),
        P(None, "sub"),
        P("sub", None),
        P(("seq", "sub"), None, None),
        P(("seq", "sub"), None, None),
        P("sub", "seq", None),
        P("sub", "seq", None),
        P(),
    )
    out_specs = P("seq", "sub")
    return jax.shard_map(body, mesh=mesh, in_specs=in_specs, out_specs=out_specs, check_vma=False)
```

profile of v0, /device:TPU:14, one launch (start us, length us, event | category | flops | bytes accessed | tf_op | source)
XLA Modules:
  0.0 213.6 jit_solution(7242579734174044836)
XLA Ops:
  6.5 0.0 copy-start
  6.5 1.0 copy.16
  7.5 0.1 eq.44
  7.6 0.1 eq.40
  7.8 1.2 reduce-window.6
  9.0 0.2 slice_reduce_fusion
  9.2 0.8 select_reduce_fusion
  10.0 0.1 reduce_sum.37
  10.2 0.1 reduce_sum.38
  10.3 0.1 copy.21
  10.4 0.3 fusion.9
  10.7 0.0 copy-done
  10.7 7.3 %convolution_convert_fusion = bf16[768,1024]{1,0:T(8,128)(2,1)} fusion(pred[768,256]{1,0:T(8,128)(4,1)S(1)} %fusion.9, bf16[256,4096]{1,0:T(8,128)(2,1)S(1)} %copy-done, bf16[4096,1024]{1,0:T(8,128)(2,1)} %param.9), kind=kOutput, calls=%fused_computation.9 | convolution fusion | flops 2551185408 | bytes 12255232 | tf_op jit(solution)/shard_map/dot_general | solution.py:32
  18.0 41.9 %all_to_all.10 = bf16[32,24,1024]{2,1,0:T(8,128)(2,1)S(1)} all-to-all(bf16[32,24,1024]{2,1,0:T(8,128)(2,1)} %bitcast.45), channel_id=1, replica_groups=mesh['seq'=8,'sub'=4] {'seq','sub'}, dimensions={0} | all-to-all | bytes 3145728 | tf_op jit(solution)/shard_map/all_to_all | solution.py:35
  59.9 0.0 copy-start.2
  59.9 5.4 %fusion = f32[768,2048]{1,0:T(8,128)S(1)} fusion(bf16[768,1024]{1,0:T(8,128)(2,1)S(1)} %bitcast.46, bf16[1,1024,2048]{2,1,0:T(8,128)(2,1)} %param.11), kind=kOutput, calls=%fused_computation.1 | convolution fusion | flops 3221225472 | bytes 12058624 | tf_op jit(solution)/shard_map/dot_general | solution.py:10
  65.3 0.0 copy-done.2
  65.3 3.0 %fusion.5 = bf16[768,1024]{1,0:T(8,128)(2,1)} fusion(bf16[1,1024,1024]{2,1,0:T(8,128)(2,1)S(1)} %copy-done.2, f32[768,2048]{1,0:T(8,128)S(1)} %fusion), kind=kOutput, calls=%fused_computation.8 | convolution fusion | flops 1616117760 | bytes 9961472 | tf_op jit(solution)/shard_map/dot_general | solution.py:13
  68.3 0.0 copy-start.1
  68.3 5.0 %all-to-all-start.1 = ((bf16[32,24,1024]{2,1,0:T(8,128)(2,1)}), bf16[32,24,1024]{2,1,0:T(8,128)(2,1)}, u32[]{:S(2)}, u32[]{:S(2)}) async-start(bf16[32,24,1024]{2,1,0:T(8,128)(2,1)} %bitcast.44), calls=%async_computation.1 | async-start | bytes 3145728 | tf_op jit(solution)/shard_map/all_to_all | solution.py:39
  73.3 0.2 reduce-scatter.2.cloned.1.call-start
  73.5 0.1 mul.52
  73.7 0.2 lt.29
  73.9 0.0 copy-done.1
  73.9 0.1 copy.19
  74.1 35.0 %all-to-all-done.1 = bf16[32,24,1024]{2,1,0:T(8,128)(2,1)} async-done(((bf16[32,24,1024]{2,1,0:T(8,128)(2,1)}), bf16[32,24,1024]{2,1,0:T(8,128)(2,1)}, u32[]{:S(2)}, u32[]{:S(2)}) %all-to-all-start.1) | async-done | bytes 1572896 | tf_op jit(solution)/shard_map/all_to_all | solution.py:39
  109.0 4.3 %gather_fusion = bf16[512,1024]{1,0:T(8,128)(2,1)S(1)} fusion(bf16[768,1024]{1,0:T(8,128)(2,1)} %bitcast.8, s32[1024]{0:T(1024)S(1)} %pad_clamp_fusion), kind=kCustom, calls=%fused_computation | custom fusion | bytes 2099200 | tf_op jit(solution)/shard_map/gather | solution.py:43
  113.4 2.4 %reshape.110 = f32[256,2,1024]{2,1,0:T(2,128)} reshape(bf16[512,1024]{1,0:T(8,128)(2,1)S(1)} %gather_fusion) | data formatting | bytes 3145728 | tf_op jit(solution)/shard_map/convert_element_type | solution.py:43
  115.8 4.3 %multiply_reduce_fusion = bf16[256,1024]{1,0:T(8,128)(2,1)S(1)} fusion(f32[256,2,1024]{2,1,0:T(2,128)} %reshape.110, f32[256,2]{1,0:T(8,128)S(1)} %bitcast_select_fusion), kind=kLoop, calls=%fused_computation.7 | loop fusion | flops 786432 | bytes 2623488 | tf_op jit(solution)/shard_map/reduce_sum | solution.py:46
  120.1 7.7 %fusion.18 = f32[256,4096]{1,0:T(8,128)} fusion(bf16[256,1024]{1,0:T(8,128)(2,1)S(1)} %multiply_reduce_fusion, bf16[1024,4096]{1,0:T(8,128)(2,1)} %param.10), kind=kOutput, calls=%fused_computation.32 | convolution fusion | flops 2147483648 | bytes 13107200 | tf_op jit(solution)/shard_map/dot_general | solution.py:47
  127.7 0.0 reduce-scatter.2.cloned.1.call-update
  127.8 76.9 %reduce-scatter.2.cloned.1.call-done = f32[256,1024]{1,0:T(8,128)} async-done(((f32[256,4096]{1,0:T(8,128)}), f32[256,1024]{1,0:T(8,128)}) %reduce-scatter.2.cloned.1.call-update) | async-done | bytes 1048592 | tf_op jit(solution)/shard_map/reduce_scatter | solution.py:48
  204.7 2.1 convert_element_type.51
  (9 shorter events, 0.1 us)
Async XLA Ops:
  6.5 4.2 %copy-start = (bf16[256,4096]{1,0:T(8,128)(2,1)S(1)}, bf16[256,4096]{1,0:T(8,128)(2,1)}, u32[]{:S(2)}) copy-start(bf16[256,4096]{1,0:T(8,128)(2,1)} %param.8) | copy-start | bytes 6291460
  59.9 5.4 %copy-start.2 = (bf16[1,1024,1024]{2,1,0:T(8,128)(2,1)S(1)}, bf16[1,1024,1024]{2,1,0:T(8,128)(2,1)}, u32[]{:S(2)}) copy-start(bf16[1,1024,1024]{2,1,0:T(8,128)(2,1)} %param.12) | copy-start | bytes 6291460
  68.3 5.6 %copy-start.1 = (s32[1,256,2]{1,2,0:T(2,128)S(1)}, s32[1,256,2]{1,2,0:T(2,128)}, u32[]{:S(2)}) copy-start(s32[1,256,2]{1,2,0:T(2,128)} %param.14) | copy-start | bytes 6148
  68.3 40.8 %all-to-all-start.1 = ((bf16[32,24,1024]{2,1,0:T(8,128)(2,1)}), bf16[32,24,1024]{2,1,0:T(8,128)(2,1)}, u32[]{:S(2)}, u32[]{:S(2)}) async-start(bf16[32,24,1024]{2,1,0:T(8,128)(2,1)} %bitcast.44), calls=%async_computation.1 | async-start | bytes 3145728 | tf_op jit(solution)/shard_map/all_to_all | solution.py:39
  73.3 131.4 %reduce-scatter.2.cloned.1.call-start = ((), (), s32[]{:S(2)}) async-start(), calls=%async_computation.3 | async-start | bytes 5242880 | tf_op jit(solution)/shard_map/reduce_scatter | solution.py:48
Sparse Core Ops, SparseCore 0:
  127.9 76.7 reduce-scatter.1
where the time goes:
time: 216 us; the launch traced here: 214 us
  waiting for transfers between devices  112 us (52%)
  blocking collectives  41.9 us (19%)
  matrix products  23.3 us (11%)
  between operations  13.6 us (6%)
  local copies, waits for them, and re-layouts  8.98 us (4%)
  other arithmetic  8.77 us (4%)
  starting transfers between devices  5.25 us (2%)
    reduce_scatter x1, waiting for transfers between devices, body(): lax.psum_scatter(partial_value, 'sub', scatter_dimension=1, tiled=True)  76.9 us
    all_to_all x1, blocking collectives, body(): lax.all_to_all(packed, ('seq', 'sub'), split_axis=0, concat_axis=0, tiled...  41.9 us
    all_to_all x1, waiting for transfers between devices, body(): lax.all_to_all(answered, ('seq', 'sub'), split_axis=0, concat_axis=0, til...  35 us
    dot_general x1, matrix products, body(): jnp.dot(head_out, w_merge, preferred_element_type=jnp.float32)  7.65 us
    dot_general x1, matrix products, body(): jnp.dot(chosen, sub_tok, preferred_element_type=jnp.float32)  7.27 us
    dot_general x1, matrix products, expert_rows(): jnp.dot(rows_flat, expert_in[0], preferred_element_type=jnp.float32)  5.39 us
    all_to_all x1, starting transfers between devices, body(): lax.all_to_all(answered, ('seq', 'sub'), split_axis=0, concat_axis=0, til...  5.03 us
    gather x1, local copies, waits for them, and re-layouts, body(): gathered = returned_rows[jnp.maximum(slot_index, 0)].astype(jnp.float32)  4.34 us
  transfers between devices with their start and end apart: 2, of which 2 were waited for; matrix products, arithmetic and copies ran while one was open for 0% of the time, Pallas kernels for 0%

commit v1 on v0

v1 whole, which is shorter than its diff:
```python
import functools

import jax
import jax.numpy as jnp
from jax import lax
from jax.experimental import pallas as pl
from jax.experimental.pallas import tpu as pltpu
from jax.sharding import PartitionSpec as P

MESH = pl.DeviceIdType.MESH
GROUPS = 4
TILE = 256
CHUNKS = 2
VMEM_LIMIT = 48 * 1024 * 1024


def experts_kernel(n_seq, n_sub, packed, w_in, w_out, returned, received, answers, hidden,
                   send_sem, recv_sem, back_sem, ret_sem):
    n = n_seq * n_sub
    me = lax.axis_index("seq") * n_sub + lax.axis_index("sub")
    block = packed.shape[0] // n
    half = packed.shape[1]
    slots = block // 2
    per = n // GROUPS
    ffe = w_out.shape[0]

    def rows(i):
        return pl.ds(pl.multiple_of(i * block, 16), block)

    def device(i):
        return (i // n_sub, lax.rem(i, n_sub))

    def outgoing(i):
        target = lax.rem(me + i, n)
        return pltpu.make_async_remote_copy(
            src_ref=packed.at[rows(target)], dst_ref=received.at[rows(i)],
            send_sem=send_sem.at[i], recv_sem=recv_sem.at[i],
            device_id=device(target), device_id_type=MESH)

    def homeward(i):
        source = lax.rem(me + n - i, n)
        return pltpu.make_async_remote_copy(
            src_ref=answers.at[rows(i)], dst_ref=returned.at[rows(me)],
            send_sem=back_sem.at[i], recv_sem=ret_sem.at[i],
            device_id=device(source), device_id_type=MESH)

    @pl.loop(1, n)
    def _(i):
        outgoing(i).start()

    received[0:block, :] = packed[rows(me), :]

    @pl.loop(0, GROUPS)
    def _(g):
        first = g * per
        low = jnp.where(g == 0, 1, first)

        @pl.loop(low, first + per)
        def _(i):
            outgoing(i).wait_recv()

        span = pl.ds(pl.multiple_of(first * block, 16), per * block)
        x = received[span, :].astype(jnp.float32).reshape(per, block, half)
        x = jnp.concatenate(
            [x[:, :slots].reshape(per * slots, half), x[:, slots:].reshape(per * slots, half)],
            axis=1).astype(jnp.bfloat16)

        @pl.loop(0, ffe // TILE)
        def _(c):
            gate_at = pl.ds(pl.multiple_of(c * TILE, TILE), TILE)
            up_at = pl.ds(pl.multiple_of(ffe + c * TILE, TILE), TILE)
            gate = jnp.dot(x, w_in[:, gate_at], preferred_element_type=jnp.float32)
            up = jnp.dot(x, w_in[:, up_at], preferred_element_type=jnp.float32)
            hidden[:, gate_at] = (gate / (1.0 + jnp.exp(-gate)) * up).astype(jnp.bfloat16)

        act = hidden[...]
        parts = []
        for h in range(2):
            y = jnp.dot(act, w_out[:, h * half:(h + 1) * half],
                        preferred_element_type=jnp.float32)
            parts.append(y.reshape(per, slots, half))
        y = jnp.concatenate(parts, axis=1).reshape(per * block, half)
        answers[span, :] = y.astype(jnp.bfloat16)

        @pl.loop(low, first + per)
        def _(i):
            homeward(i).start()

    returned[rows(me), :] = answers[0:block, :]

    @pl.loop(1, n)
    def _(i):
        outgoing(i).wait_send()
        homeward(i).wait_send()
        homeward(i).wait_recv()


def exchange_experts(n_seq, n_sub, packed, w_in, w_out):
    n = n_seq * n_sub
    width = w_out.shape[0]
    vmem = pl.BlockSpec(memory_space=pltpu.VMEM)
    rows = packed.shape[0] // 2 // GROUPS
    return pl.pallas_call(
        functools.partial(experts_kernel, n_seq, n_sub),
        out_shape=jax.ShapeDtypeStruct(packed.shape, jnp.bfloat16),
        in_specs=[vmem] * 3,
        out_specs=vmem,
        scratch_shapes=[
            pltpu.VMEM(packed.shape, jnp.bfloat16),
            pltpu.VMEM(packed.shape, jnp.bfloat16),
            pltpu.VMEM((rows, width), jnp.bfloat16),
        ] + [pltpu.SemaphoreType.DMA((n,))] * 4,
        compiler_params=pltpu.CompilerParams(has_side_effects=True, vmem_limit_bytes=VMEM_LIMIT),
        name="experts",
    )(packed, w_in, w_out)


def merge_kernel(n, head, w_hbm, out, w, total, sending, landed, w_sem, send_sem, recv_sem):
    z = lax.axis_index("sub")
    rows, width = out.shape
    piece = rows // CHUNKS

    def target(j):
        near_low = jnp.where(j < n - 1 - z, n - 1 - j, j - (n - 1 - z))
        near_high = jnp.where(j < z, j, n - 1 - (j - z))
        return jnp.where(z < n // 2, near_low, near_high)

    def fetch(j):
        t = target(j)
        return pltpu.make_async_copy(
            w_hbm.at[:, pl.ds(pl.multiple_of(t * width, width), width)], w.at[t], w_sem.at[j])

    for j in range(n):
        fetch(j).start()

    barrier = pltpu.get_barrier_semaphore()

    @pl.when(z > 0)
    def _():
        pl.semaphore_signal(barrier, inc=1, device_id={"sub": z - 1}, device_id_type=MESH)

    @pl.when(z < n - 1)
    def _():
        pl.semaphore_signal(barrier, inc=1, device_id={"sub": z + 1}, device_id_type=MESH)

    pl.semaphore_wait(barrier, jnp.where(z > 0, 1, 0) + jnp.where(z < n - 1, 1, 0))

    def hop(way, t, c):
        part = pl.ds(c * piece, piece)
        return pltpu.make_async_remote_copy(
            src_ref=sending.at[t, part], dst_ref=landed.at[way, t, part],
            send_sem=send_sem.at[t, c], recv_sem=recv_sem.at[way, t, c],
            device_id={"sub": z + (1 if way == 0 else -1)}, device_id_type=MESH)

    for j in range(n):
        t = target(j)
        fetch(j).wait()

        @pl.loop(0, width // TILE)
        def _(k):
            cols = pl.ds(pl.multiple_of(k * TILE, TILE), TILE)
            total[t, :, cols] = jnp.dot(head[...], w[t, :, cols],
                                        preferred_element_type=jnp.float32)

        for way, source in ((0, 0), (1, n - 1)):
            @pl.when((z == source) & (t != z))
            def _():
                for c in range(CHUNKS):
                    part = pl.ds(c * piece, piece)
                    sending[t, part, :] = total[t, part, :].astype(jnp.bfloat16)
                    hop(way, t, c).start()

    for k in range(n - 2):
        for c in range(CHUNKS):
            part = pl.ds(c * piece, piece)
            for way, t in ((0, n - 1 - k), (1, k)):
                inside = (z > 0) & (z < t) if way == 0 else (z < n - 1) & (z > t)

                @pl.when(inside)
                def _():
                    hop(way, t, c).wait_recv()
                    sending[t, part, :] = (
                        total[t, part, :] + landed[way, t, part, :].astype(jnp.float32)
                    ).astype(jnp.bfloat16)
                    hop(way, t, c).start()

    for way, has in ((0, z > 0), (1, z < n - 1)):
        @pl.when(has)
        def _():
            for c in range(CHUNKS):
                part = pl.ds(c * piece, piece)
                hop(way, z, c).wait_recv()
                total[z, part, :] += landed[way, z, part, :].astype(jnp.float32)

    out[...] = total[z].astype(out.dtype)
    for t in range(n):
        @pl.when(z < t)
        def _():
            for c in range(CHUNKS):
                hop(0, t, c).wait_send()

        @pl.when(z > t)
        def _():
            for c in range(CHUNKS):
                hop(1, t, c).wait_send()


def merge_scatter(n, head, w_merge):
    rows, width = head.shape[0], w_merge.shape[1] // n
    depth = w_merge.shape[0]
    vmem = pl.BlockSpec(memory_space=pltpu.VMEM)
    return pl.pallas_call(
        functools.partial(merge_kernel, n),
        out_shape=jax.ShapeDtypeStruct((rows, width), jnp.bfloat16),
        in_specs=[vmem, pl.BlockSpec(memory_space=pl.ANY)],
        out_specs=vmem,
        scratch_shapes=[
            pltpu.VMEM((n, depth, width), jnp.bfloat16),
            pltpu.VMEM((n, rows, width), jnp.float32),
            pltpu.VMEM((n, rows, width), jnp.bfloat16),
            pltpu.VMEM((2, n, rows, width), jnp.bfloat16),
            pltpu.SemaphoreType.DMA((n,)),
            pltpu.SemaphoreType.DMA((n, CHUNKS)),
            pltpu.SemaphoreType.DMA((2, n, CHUNKS)),
        ],
        compiler_params=pltpu.CompilerParams(
            collective_id=1, has_side_effects=True, vmem_limit_bytes=VMEM_LIMIT),
        name="merge",
    )(head, w_merge)


def body(n_seq, n_sub, tokens, w_split, w_merge, expert_in, expert_out, expert_ids, combine_q,
         capacity):
    sub_tok = jnp.dot(tokens, w_split, preferred_element_type=jnp.float32).astype(jnp.bfloat16)
    tok_rows = tokens.shape[0]
    experts = capacity.shape[0]
    slot_count = -(-(3 * tok_rows // experts) // 8) * 8
    expert_of = expert_ids[0].reshape(-1)
    onehot = (expert_of[:, None] == jnp.arange(experts, dtype=jnp.int32)[None, :]).astype(jnp.int32)
    order_rank = jnp.sum((jnp.cumsum(onehot, axis=0) - onehot) * onehot, axis=1)
    cap_limit = jnp.sum(onehot * capacity[None, :], axis=1)
    is_kept = order_rank < cap_limit
    place = jnp.where(is_kept, expert_of * (2 * slot_count) + order_rank, -(4 * slot_count))
    place = place.reshape(tok_rows, -1)
    half = sub_tok.shape[1] // 2
    target = jnp.arange(experts * 2 * slot_count, dtype=jnp.int32)
    both = jnp.concatenate([place, place + slot_count], axis=0)
    chosen = (
        (target[:, None] == both[None, :, 0]) | (target[:, None] == both[None, :, 1])
    ).astype(jnp.bfloat16)
    stacked = jnp.concatenate([sub_tok[:, :half], sub_tok[:, half:]], axis=0)
    packed = jnp.dot(chosen, stacked, preferred_element_type=jnp.float32).astype(jnp.bfloat16)
    returned = exchange_experts(n_seq, n_sub, packed, expert_in[0], expert_out[0])
    weight = combine_q[0].astype(jnp.float32) / 65536.0
    twice = jnp.concatenate([weight, weight], axis=0)
    spread = (
        jnp.where(both[:, 0:1] == target[None, :], twice[:, 0:1], 0.0)
        + jnp.where(both[:, 1:2] == target[None, :], twice[:, 1:2], 0.0)
    )
    high = spread.astype(jnp.bfloat16)
    low = (spread - high.astype(jnp.float32)).astype(jnp.bfloat16)
    summed = (jnp.dot(high, returned, preferred_element_type=jnp.float32)
              + jnp.dot(low, returned, preferred_element_type=jnp.float32))
    head_out = jnp.concatenate([summed[:tok_rows], summed[tok_rows:]], axis=1).astype(jnp.bfloat16)
    return merge_scatter(n_sub, head_out, w_merge)


def solution(mesh):
    in_specs = (
        P("seq", None),
        P(None, "sub"),
        P("sub", None),
        P(("seq", "sub"), None, None),
        P(("seq", "sub"), None, None),
        P("sub", "seq", None),
        P("sub", "seq", None),
        P(),
    )
    out_specs = P("seq", "sub")
    call = functools.partial(body, mesh.shape["seq"], mesh.shape["sub"])
    return jax.shard_map(call, mesh=mesh, in_specs=in_specs, out_specs=out_specs, check_vma=False)
```

time: 216 us -> 143 us (0.66); the launches traced: 214 us -> 143 us
  Pallas kernels: 0 us -> 127 us
  waiting for transfers between devices: 112 us -> 0 us
  blocking collectives: 41.9 us -> 0 us
  matrix products: 23.3 us -> 9.39 us
  between operations: 13.6 us -> 0.13 us
  local copies, waits for them, and re-layouts: 8.98 us -> 3.19 us
  starting transfers between devices: 5.25 us -> 0 us
  other arithmetic: 8.77 us -> 3.59 us
    pallas_call x0 -> x2, Pallas kernels: none -> 127 us  [the longest x1 77.4 us: exchange_experts(): pl.pallas_call(functools.partial(experts_kernel, n_seq, n_sub), out_shape...]
    reduce_scatter x1 -> x0, waiting for transfers between devices: 76.9 us -> none  [body(): lax.psum_scatter(partial_value, 'sub', scatter_dimension=1, tiled=True)]
    all_to_all x1 -> x0, blocking collectives: 41.9 us -> none  [body(): lax.all_to_all(packed, ('seq', 'sub'), split_axis=0, concat_axis=0, tiled...]
    all_to_all x1 -> x0, waiting for transfers between devices: 35 us -> none  [body(): lax.all_to_all(answered, ('seq', 'sub'), split_axis=0, concat_axis=0, til...]
    dot_general x4, matrix products: 23.3 us -> 9.39 us  [the longest x1 5.71 us: body(): jnp.dot(tokens, w_split, preferred_element_type=jnp.float32)]
    all_to_all x1 -> x0, starting transfers between devices: 5.03 us -> none  [body(): lax.all_to_all(answered, ('seq', 'sub'), split_axis=0, concat_axis=0, til...]
    gather x1 -> x0, local copies, waits for them, and re-layouts: 4.34 us -> none  [body(): gathered = returned_rows[jnp.maximum(slot_index, 0)].astype(jnp.float32)]
    reduce_sum x1 -> x0, other arithmetic: 4.33 us -> none  [body(): head_out = jnp.sum(weighted, axis=1).astype(jnp.bfloat16)]
  transfers between devices with their start and end apart: 2 -> 0, of which waited for: 2 -> 0; matrix products, arithmetic and copies ran while one was open for 0% -> 0% of each run, Pallas kernels for 0% -> 0%
where the time goes in v1:
time: 143 us
  Pallas kernels  127 us (89%)
  matrix products  9.39 us (7%)
  other arithmetic  3.59 us (3%)
  local copies, waits for them, and re-layouts  3.19 us (2%)
    pallas_call x1, Pallas kernels, exchange_experts(): pl.pallas_call(functools.partial(experts_kernel, n_seq, n_sub), out_shape...  77.4 us
    pallas_call x1, Pallas kernels, merge_scatter(): pl.pallas_call(functools.partial(merge_kernel, n), out_shape=jax.ShapeDty...  49.2 us
    dot_general x1, matrix products, body(): jnp.dot(tokens, w_split, preferred_element_type=jnp.float32)  5.71 us

profile of v1, /device:TPU:14, one launch (start us, length us, event | category | flops | bytes accessed | tf_op | source)
XLA Modules:
  0.0 142.9 jit_solution(7091320059407128493)
XLA Ops:
  0.0 0.0 copy-start
  0.0 0.8 multiply_bitcast_fusion
  0.8 0.8 copy.32
  1.7 0.1 eq.85
  1.8 0.1 eq.81
  2.0 1.2 reduce-window.6
  3.1 0.2 slice_reduce_fusion
  3.4 0.8 select_reduce_fusion
  4.2 0.1 reduce_sum.25
  4.3 0.1 copy.36
  4.4 0.1 reduce_sum.23
  4.6 0.1 copy.35
  4.6 0.7 broadcast_add_fusion
  5.3 0.0 copy-done
  5.3 5.7 %convolution_convert_fusion = bf16[256,1024]{1,0:T(8,128)(2,1)S(1)} fusion(bf16[256,4096]{1,0:T(8,128)(2,1)S(1)} %copy-done, bf16[4096,1024]{1,0:T(8,128)(2,1)} %param.9), kind=kOutput, calls=%fused_computation.21 | convolution fusion | flops 2147745792 | bytes 11010048 | tf_op jit(solution)/shard_map/dot_general | solution.py:234
  11.1 0.0 copy-start.1
  11.1 1.0 fusion.4.packed
  12.1 0.6 copy-done.1
  12.7 77.4 %experts.1 = bf16[1536,512]{1,0:T(8,128)(2,1)S(1)} custom-call(bf16[1536,512]{1,0:T(8,128)(2,1)S(1)} %fusion.4.packed, bf16[1024,2048]{1,0:T(8,128)(2,1)} %bitcast.37, bf16[1024,1024]{1,0:T(8,128)(2,1)S(1)} %bitcast.36), custom_call_target="tpu_custom_call" | custom-call | tf_op jit(solution)/shard_map/experts/pallas_call | solution.py:103
  90.1 1.2 fusion.16
  91.3 1.5 %fusion.19 = bf16[512,512]{1,0:T(8,128)(2,1)S(1)} fusion(f32[512,512]{1,0:T(8,128)S(1)} %fusion.16, bf16[1536,512]{1,0:T(8,128)(2,1)S(1)} %experts.1, f32[512]{0:T(512)S(1)} %bitcast.41, s32[512]{0:T(512)S(1)} %bitcast.47, f32[512]{0:T(512)S(1)} %bitcast.39, s32[512]{0:T(512)S(1)} %bitcast.44), kind=kOutput, calls=%fused_computation.20 | convolution fusion | flops 812908544 | bytes 3153920 | tf_op jit(solution)/shard_map/dot_general | solution.py:263
  92.9 0.1 pad_maximum_fusion.head
  92.9 49.2 %merge.1 = bf16[256,1024]{1,0:T(8,128)(2,1)S(1)} custom-call(bf16[256,1024]{1,0:T(8,128)(2,1)S(1)} %pad_maximum_fusion.head, bf16[1024,4096]{1,0:T(8,128)(2,1)} %w_hbm.1), custom_call_target="tpu_custom_call" | custom-call | tf_op jit(solution)/shard_map/merge/pallas_call | solution.py:212
  142.1 0.8 copy.45
  (7 shorter events, 0.1 us)
Async XLA Ops:
  0.0 5.3 %copy-start = (bf16[256,4096]{1,0:T(8,128)(2,1)S(1)}, bf16[256,4096]{1,0:T(8,128)(2,1)}, u32[]{:S(2)}) copy-start(bf16[256,4096]{1,0:T(8,128)(2,1)} %param.8) | copy-start | bytes 6291460
  11.1 1.6 %copy-start.1 = (bf16[1,1024,1024]{2,1,0:T(8,128)(2,1)S(1)}, bf16[1,1024,1024]{2,1,0:T(8,128)(2,1)}, u32[]{:S(2)}) copy-start(bf16[1,1024,1024]{2,1,0:T(8,128)(2,1)} %param.12) | copy-start | bytes 6291460

commit v2 on v1

v2 whole, which is shorter than its diff:
```python
import functools

import jax
import jax.numpy as jnp
from jax import lax
from jax.experimental import pallas as pl
from jax.experimental.pallas import tpu as pltpu
from jax.sharding import PartitionSpec as P

MESH = pl.DeviceIdType.MESH
GROUPS = 4
TILE = 256
CHUNKS = 2
EXPERTS_VMEM = 28 * 1024 * 1024
MERGE_VMEM = 28 * 1024 * 1024


def experts_kernel(n_seq, n_sub, slots, sub_tok, ids, quanta, capacity, w_in_hbm, w_out_hbm, head,
                   packed, received, answers, returned, hidden, w_in, w_out, w_sem,
                   send_sem, recv_sem, back_sem, ret_sem):
    n = n_seq * n_sub
    me = lax.axis_index("seq") * n_sub + lax.axis_index("sub")
    tok_rows, width = sub_tok.shape
    half = width // 2
    block = 2 * slots
    per = n // GROUPS
    ffe = w_out.shape[0]

    fetch_in = pltpu.make_async_copy(w_in_hbm, w_in, w_sem.at[0])
    fetch_out = pltpu.make_async_copy(w_out_hbm, w_out, w_sem.at[1])

    def rows(i):
        return pl.ds(pl.multiple_of(i * block, 16), block)

    def span(g):
        return pl.ds(pl.multiple_of(g * per * block, 16), per * block)

    def device(i):
        return (i // n_sub, lax.rem(i, n_sub))

    def outgoing(i):
        return pltpu.make_async_remote_copy(
            src_ref=packed.at[rows(i)], dst_ref=received.at[rows(i)],
            send_sem=send_sem.at[i], recv_sem=recv_sem.at[i],
            device_id=device(lax.rem(me + i, n)), device_id_type=MESH)

    def homeward(i):
        return pltpu.make_async_remote_copy(
            src_ref=answers.at[rows(i)], dst_ref=returned.at[rows(i)],
            send_sem=back_sem.at[i], recv_sem=ret_sem.at[i],
            device_id=device(lax.rem(me + n - i, n)), device_id_type=MESH)

    def fold(y):
        y = y.reshape(per, slots, width)
        y = jnp.concatenate([y[:, :, :half], y[:, :, half:]], axis=1)
        return y.reshape(per * block, half).astype(jnp.bfloat16)

    def unfold(x):
        x = x.astype(jnp.float32).reshape(per, block, half)
        return jnp.concatenate(
            [x[:, :slots].reshape(per * slots, half), x[:, slots:].reshape(per * slots, half)],
            axis=1).astype(jnp.bfloat16)

    places = lax.broadcasted_iota(jnp.int32, (n, tok_rows), 0)
    named = [(places == ids[k:k + 1, :]).astype(jnp.float32) for k in range(2)]
    before = (lax.broadcasted_iota(jnp.int32, (tok_rows, tok_rows), 0)
              < lax.broadcasted_iota(jnp.int32, (tok_rows, tok_rows), 1))
    earlier = jnp.dot((named[0] + named[1]).astype(jnp.bfloat16),
                      before.astype(jnp.float32).astype(jnp.bfloat16),
                      preferred_element_type=jnp.float32)
    limit = capacity[...].astype(jnp.float32)
    slot, weight = [], []
    for k in range(2):
        rank = jnp.sum(named[k] * earlier, axis=0, keepdims=True)
        most = jnp.sum(named[k] * limit, axis=0, keepdims=True)
        away = ids[k:k + 1, :] - me
        away = jnp.where(away < 0, away + n, away)
        slot.append(jnp.where(rank < most, away * slots + rank.astype(jnp.int32), -1))
        weight.append(quanta[k:k + 1, :].astype(jnp.float32) / 65536.0)

    def spread(g, values):
        at = lax.broadcasted_iota(jnp.int32, (per * slots, tok_rows), 0) + g * (per * slots)
        return (jnp.where(at == slot[0], values[0], 0.0)
                + jnp.where(at == slot[1], values[1], 0.0))

    for g in range(GROUPS):
        chosen = spread(g, (1.0, 1.0)).astype(jnp.bfloat16)
        packed[span(g), :] = fold(jnp.dot(chosen, sub_tok[...],
                                          preferred_element_type=jnp.float32))

        @pl.loop(max(1, g * per), (g + 1) * per)
        def _(i):
            outgoing(i).start()

        if g == 0:
            fetch_in.start()
            fetch_out.start()

    received[0:block, :] = packed[0:block, :]
    fetch_in.wait()
    fetch_out.wait()

    @pl.loop(0, GROUPS)
    def _(g):
        first = g * per
        low = jnp.where(g == 0, 1, first)

        @pl.loop(low, first + per)
        def _(i):
            outgoing(i).wait_recv()

        x = unfold(received[span(g), :])

        @pl.loop(0, ffe // TILE)
        def _(c):
            gate_at = pl.ds(pl.multiple_of(c * TILE, TILE), TILE)
            up_at = pl.ds(pl.multiple_of(ffe + c * TILE, TILE), TILE)
            gate = jnp.dot(x, w_in[:, gate_at], preferred_element_type=jnp.float32)
            up = jnp.dot(x, w_in[:, up_at], preferred_element_type=jnp.float32)
            hidden[:, gate_at] = (gate / (1.0 + jnp.exp(-gate)) * up).astype(jnp.bfloat16)

        act = hidden[...]
        parts = []
        for h in range(2):
            y = jnp.dot(act, w_out[:, h * half:(h + 1) * half],
                        preferred_element_type=jnp.float32)
            parts.append(y.reshape(per, slots, half))
        y = jnp.concatenate(parts, axis=1).reshape(per * block, half)
        answers[span(g), :] = y.astype(jnp.bfloat16)

        @pl.loop(low, first + per)
        def _(i):
            homeward(i).start()

    returned[0:block, :] = answers[0:block, :]
    summed = jnp.zeros((tok_rows, width), jnp.float32)
    for g in range(GROUPS):
        @pl.loop(max(1, g * per), (g + 1) * per)
        def _(i):
            homeward(i).wait_recv()

        full = spread(g, weight)
        high = full.astype(jnp.bfloat16)
        low = (full - high.astype(jnp.float32)).astype(jnp.bfloat16)
        y = unfold(returned[span(g), :])
        for part in (high, low):
            summed = summed + lax.dot_general(part, y, (((0,), (0,)), ((), ())),
                                              preferred_element_type=jnp.float32)
    head[...] = summed.astype(jnp.bfloat16)

    @pl.loop(1, n)
    def _(i):
        outgoing(i).wait_send()
        homeward(i).wait_send()


def exchange_experts(n_seq, n_sub, slots, sub_tok, ids, quanta, capacity, w_in, w_out):
    n = n_seq * n_sub
    width = w_out.shape[1]
    vmem = pl.BlockSpec(memory_space=pltpu.VMEM)
    hbm = pl.BlockSpec(memory_space=pltpu.HBM)
    rows = n * slots // GROUPS
    crossing = pltpu.VMEM((n * 2 * slots, width // 2), jnp.bfloat16)
    return pl.pallas_call(
        functools.partial(experts_kernel, n_seq, n_sub, slots),
        out_shape=jax.ShapeDtypeStruct(sub_tok.shape, jnp.bfloat16),
        in_specs=[vmem] * 4 + [hbm] * 2,
        out_specs=vmem,
        scratch_shapes=[crossing] * 4 + [
            pltpu.VMEM((rows, w_out.shape[0]), jnp.bfloat16),
            pltpu.VMEM(w_in.shape, jnp.bfloat16),
            pltpu.VMEM(w_out.shape, jnp.bfloat16),
            pltpu.SemaphoreType.DMA((2,)),
        ] + [pltpu.SemaphoreType.DMA((n,))] * 4,
        compiler_params=pltpu.CompilerParams(
            has_side_effects=True, vmem_limit_bytes=EXPERTS_VMEM),
        name="experts",
    )(sub_tok, ids, quanta, capacity, w_in, w_out)


def merge_kernel(n, head, w, out, total, sending, landed, send_sem, recv_sem):
    z = lax.axis_index("sub")
    rows, width = out.shape
    piece = rows // CHUNKS

    def target(j):
        near_low = jnp.where(j < n - 1 - z, n - 1 - j, j - (n - 1 - z))
        near_high = jnp.where(j < z, j, n - 1 - (j - z))
        return jnp.where(z < n // 2, near_low, near_high)

    barrier = pltpu.get_barrier_semaphore()

    @pl.when(z > 0)
    def _():
        pl.semaphore_signal(barrier, inc=1, device_id={"sub": z - 1}, device_id_type=MESH)

    @pl.when(z < n - 1)
    def _():
        pl.semaphore_signal(barrier, inc=1, device_id={"sub": z + 1}, device_id_type=MESH)

    pl.semaphore_wait(barrier, jnp.where(z > 0, 1, 0) + jnp.where(z < n - 1, 1, 0))

    def hop(way, t, c):
        part = pl.ds(c * piece, piece)
        return pltpu.make_async_remote_copy(
            src_ref=sending.at[t, part], dst_ref=landed.at[way, t, part],
            send_sem=send_sem.at[t, c], recv_sem=recv_sem.at[way, t, c],
            device_id={"sub": z + (1 if way == 0 else -1)}, device_id_type=MESH)

    for j in range(n):
        t = target(j)

        @pl.loop(0, width // TILE)
        def _(k):
            cols = pl.ds(pl.multiple_of(k * TILE, TILE), TILE)
            from_cols = pl.ds(pl.multiple_of(t * width + k * TILE, TILE), TILE)
            total[t, :, cols] = jnp.dot(head[...], w[:, from_cols],
                                        preferred_element_type=jnp.float32)

        for way, source in ((0, 0), (1, n - 1)):
            @pl.when((z == source) & (t != z))
            def _():
                for c in range(CHUNKS):
                    part = pl.ds(c * piece, piece)
                    sending[t, part, :] = total[t, part, :].astype(jnp.bfloat16)
                    hop(way, t, c).start()

    for k in range(n - 2):
        for c in range(CHUNKS):
            part = pl.ds(c * piece, piece)
            for way, t in ((0, n - 1 - k), (1, k)):
                inside = (z > 0) & (z < t) if way == 0 else (z < n - 1) & (z > t)

                @pl.when(inside)
                def _():
                    hop(way, t, c).wait_recv()
                    sending[t, part, :] = (
                        total[t, part, :] + landed[way, t, part, :].astype(jnp.float32)
                    ).astype(jnp.bfloat16)
                    hop(way, t, c).start()

    for way, has in ((0, z > 0), (1, z < n - 1)):
        @pl.when(has)
        def _():
            for c in range(CHUNKS):
                part = pl.ds(c * piece, piece)
                hop(way, z, c).wait_recv()
                total[z, part, :] += landed[way, z, part, :].astype(jnp.float32)

    out[...] = total[z].astype(out.dtype)
    for t in range(n):
        @pl.when(z < t)
        def _():
            for c in range(CHUNKS):
                hop(0, t, c).wait_send()

        @pl.when(z > t)
        def _():
            for c in range(CHUNKS):
                hop(1, t, c).wait_send()


def merge_scatter(n, head, w_merge):
    rows, width = head.shape[0], w_merge.shape[1] // n
    vmem = pl.BlockSpec(memory_space=pltpu.VMEM)
    return pl.pallas_call(
        functools.partial(merge_kernel, n),
        out_shape=jax.ShapeDtypeStruct((rows, width), jnp.bfloat16),
        in_specs=[vmem, vmem],
        out_specs=vmem,
        scratch_shapes=[
            pltpu.VMEM((n, rows, width), jnp.float32),
            pltpu.VMEM((n, rows, width), jnp.bfloat16),
            pltpu.VMEM((2, n, rows, width), jnp.bfloat16),
            pltpu.SemaphoreType.DMA((n, CHUNKS)),
            pltpu.SemaphoreType.DMA((2, n, CHUNKS)),
        ],
        compiler_params=pltpu.CompilerParams(
            collective_id=1, has_side_effects=True, vmem_limit_bytes=MERGE_VMEM),
        name="merge",
    )(head, w_merge)


def body(n_seq, n_sub, tokens, w_split, w_merge, expert_in, expert_out, expert_ids, combine_q,
         capacity):
    sub_tok = jnp.dot(tokens, w_split, preferred_element_type=jnp.float32).astype(jnp.bfloat16)
    sub_tok, w_merge = lax.optimization_barrier((sub_tok, w_merge))
    tok_rows = tokens.shape[0]
    experts = capacity.shape[0]
    slot_count = -(-(3 * tok_rows // experts) // 8) * 8
    head_out = exchange_experts(
        n_seq, n_sub, slot_count, sub_tok, expert_ids[0].T, combine_q[0].T, capacity[:, None],
        expert_in[0], expert_out[0])
    return merge_scatter(n_sub, head_out, w_merge)


def solution(mesh):
    in_specs = (
        P("seq", None),
        P(None, "sub"),
        P("sub", None),
        P(("seq", "sub"), None, None),
        P(("seq", "sub"), None, None),
        P("sub", "seq", None),
        P("sub", "seq", None),
        P(),
    )
    out_specs = P("seq", "sub")
    call = functools.partial(body, mesh.shape["seq"], mesh.shape["sub"])
    return jax.shard_map(call, mesh=mesh, in_specs=in_specs, out_specs=out_specs, check_vma=False)
```

time: 143 us -> 133 us (0.930)
  other arithmetic: 3.59 us -> 0 us
  matrix products: 9.39 us -> 5.86 us
  Pallas kernels: 127 us -> 124 us
    dot_general x3 -> x0, matrix products: 3.68 us -> none  [the longest x1 1.49 us: body(): jnp.dot(low, returned, preferred_element_type=jnp.float32)]
    pallas_call x1, Pallas kernels: 49.2 us -> 47.5 us  [merge_scatter(): pl.pallas_call(functools.partial(merge_kernel, n), out_shape=jax.ShapeDty...]
where the time goes in v2:
time: 133 us; the launch traced here: 132 us
  Pallas kernels  124 us (93%)
  matrix products  5.86 us (4%)
  local copies, waits for them, and re-layouts  2.42 us (2%)
    pallas_call x1, Pallas kernels, exchange_experts(): pl.pallas_call(functools.partial(experts_kernel, n_seq, n_sub, slots), ou...  76.5 us
    pallas_call x1, Pallas kernels, merge_scatter(): pl.pallas_call(functools.partial(merge_kernel, n), out_shape=jax.ShapeDty...  47.5 us
    dot_general x1, matrix products, body(): jnp.dot(tokens, w_split, preferred_element_type=jnp.float32)  5.86 us

profile of v2, /device:TPU:14, one launch (start us, length us, event | category | flops | bytes accessed | tf_op | source)
XLA Modules:
  0.0 132.4 jit_solution(8517262471581541329)
XLA Ops:
  0.0 0.0 copy-start
  0.0 0.9 copy.9.capacity
  0.9 0.7 copy-done
  1.6 0.0 copy-start.2
  1.6 0.0 copy-start.3
  1.6 0.0 copy-start.4
  1.6 0.0 copy-start.5
  1.6 0.0 copy-start.1
  1.6 5.9 %convolution_convert_fusion.sub_tok = bf16[256,1024]{1,0:T(8,128)(2,1)S(1)} fusion(bf16[256,4096]{1,0:T(8,128)(2,1)S(1)} %copy-done, bf16[4096,1024]{1,0:T(8,128)(2,1)} %param.9), kind=kOutput, calls=%fused_computation | convolution fusion | flops 2147745792 | bytes 11010048 | tf_op jit(solution)/shard_map/dot_general | solution.py:286
  7.5 0.0 copy-done.2
  7.5 0.0 copy-done.3
  7.5 0.0 copy-done.4
  7.5 0.0 copy-done.5
  7.5 76.5 %experts.1.head = bf16[256,1024]{1,0:T(8,128)(2,1)S(1)} custom-call(bf16[256,1024]{1,0:T(8,128)(2,1)S(1)} %convolution_convert_fusion.sub_tok, s32[2,256]{1,0:T(2,128)S(1)} %bitcast.13, s32[2,256]{1,0:T(2,128)S(1)} %bitcast.14, s32[32,1]{1,0:T(8,128)S(1)} %copy.9.capacity, bf16[1024,2048]{1,0:T(8,128)(2,1)S(1)} %bitcast.11, bf16[1024,1024]{1,0:T(8,128)(2,1)S(1)} %bitcast.12), custom_call_target="tpu_custom_call" | custom-call | tf_op jit(solution)/shard_map/experts/pallas_call | solution.py:164
  84.0 0.0 copy-done.1
  84.0 47.5 %merge.1 = bf16[256,1024]{1,0:T(8,128)(2,1)S(1)} custom-call(bf16[256,1024]{1,0:T(8,128)(2,1)S(1)} %experts.1.head, bf16[1024,4096]{1,0:T(8,128)(2,1)S(1)} %copy-done.1), custom_call_target="tpu_custom_call" | custom-call | tf_op jit(solution)/shard_map/merge/pallas_call | solution.py:266
  131.6 0.8 copy.11
Async XLA Ops:
  0.0 1.6 %copy-start = (bf16[256,4096]{1,0:T(8,128)(2,1)S(1)}, bf16[256,4096]{1,0:T(8,128)(2,1)}, u32[]{:S(2)}) copy-start(bf16[256,4096]{1,0:T(8,128)(2,1)} %param.8) | copy-start | bytes 6291460
  1.6 5.9 %copy-start.2 = (bf16[1,1024,2048]{2,1,0:T(8,128)(2,1)S(1)}, bf16[1,1024,2048]{2,1,0:T(8,128)(2,1)}, u32[]{:S(2)}) copy-start(bf16[1,1024,2048]{2,1,0:T(8,128)(2,1)} %param.11) | copy-start | bytes 12582916
  1.6 5.9 %copy-start.3 = (bf16[1,1024,1024]{2,1,0:T(8,128)(2,1)S(1)}, bf16[1,1024,1024]{2,1,0:T(8,128)(2,1)}, u32[]{:S(2)}) copy-start(bf16[1,1024,1024]{2,1,0:T(8,128)(2,1)} %param.12) | copy-start | bytes 6291460
  1.6 5.9 %copy-start.4 = (s32[1,256,2]{1,2,0:T(2,128)S(1)}, s32[1,256,2]{1,2,0:T(2,128)}, u32[]{:S(2)}) copy-start(s32[1,256,2]{1,2,0:T(2,128)} %param.13) | copy-start | bytes 6148
  1.6 5.9 %copy-start.5 = (s32[1,256,2]{1,2,0:T(2,128)S(1)}, s32[1,256,2]{1,2,0:T(2,128)}, u32[]{:S(2)}) copy-start(s32[1,256,2]{1,2,0:T(2,128)} %param.14) | copy-start | bytes 6148
  1.6 82.4 %copy-start.1 = (bf16[1024,4096]{1,0:T(8,128)(2,1)S(1)}, bf16[1024,4096]{1,0:T(8,128)(2,1)}, u32[]{:S(2)}) copy-start(bf16[1024,4096]{1,0:T(8,128)(2,1)} %w) | copy-start | bytes 25165828

commit v3 on v2

--- a/solution.py
+++ b/solution.py
@@ -68,7 +68,10 @@
     earlier = jnp.dot((named[0] + named[1]).astype(jnp.bfloat16),
                       before.astype(jnp.float32).astype(jnp.bfloat16),
                       preferred_element_type=jnp.float32)
-    limit = capacity[...].astype(jnp.float32)
+    square = lax.broadcasted_iota(jnp.int32, (n, n), 0)
+    across = lax.broadcasted_iota(jnp.int32, (n, n), 1)
+    limit = jnp.sum(jnp.where(square == across, capacity[...].astype(jnp.float32), 0.0),
+                    axis=1, keepdims=True)
     slot, weight = [], []
     for k in range(2):
         rank = jnp.sum(named[k] * earlier, axis=0, keepdims=True)
@@ -209,35 +212,43 @@
 
     for j in range(n):
         t = target(j)
-
-        @pl.loop(0, width // TILE)
-        def _(k):
-            cols = pl.ds(pl.multiple_of(k * TILE, TILE), TILE)
-            from_cols = pl.ds(pl.multiple_of(t * width + k * TILE, TILE), TILE)
-            total[t, :, cols] = jnp.dot(head[...], w[:, from_cols],
-                                        preferred_element_type=jnp.float32)
-
-        for way, source in ((0, 0), (1, n - 1)):
-            @pl.when((z == source) & (t != z))
+        steps = 2 if j == 0 else 1
+        for step in range(steps):
+            tall = pl.ds(step * (rows // steps), rows // steps)
+
+            @pl.loop(0, width // TILE)
+            def _(k):
+                cols = pl.ds(pl.multiple_of(k * TILE, TILE), TILE)
+                from_cols = pl.ds(pl.multiple_of(t * width + k * TILE, TILE), TILE)
+                total[t, tall, cols] = jnp.dot(head[tall, :], w[:, from_cols],
+                                               preferred_element_type=jnp.float32)
+
+            for way, source in ((0, 0), (1, n - 1)):
+                @pl.when((z == source) & (t != z))
+                def _():
+                    for c in range(step * CHUNKS // steps, (step + 1) * CHUNKS // steps):
+                        part = pl.ds(c * piece, piece)
+                        sending[t, part, :] = total[t, part, :].astype(jnp.bfloat16)
+                        hop(way, t, c).start()
+
+    def relay(way, when):
+        for k in range(n - 2):
+            t = n - 1 - k if way == 0 else k
+            inside = (z > 0) & (z < t) if way == 0 else (z < n - 1) & (z > t)
+
+            @pl.when(inside & when)
             def _():
                 for c in range(CHUNKS):
                     part = pl.ds(c * piece, piece)
-                    sending[t, part, :] = total[t, part, :].astype(jnp.bfloat16)
-                    hop(way, t, c).start()
-
-    for k in range(n - 2):
-        for c in range(CHUNKS):
-            part = pl.ds(c * piece, piece)
-            for way, t in ((0, n - 1 - k), (1, k)):
-                inside = (z > 0) & (z < t) if way == 0 else (z < n - 1) & (z > t)
-
-                @pl.when(inside)
-                def _():
                     hop(way, t, c).wait_recv()
                     sending[t, part, :] = (
                         total[t, part, :] + landed[way, t, part, :].astype(jnp.float32)
                     ).astype(jnp.bfloat16)
                     hop(way, t, c).start()
+
+    relay(0, z < n // 2)
+    relay(1, z >= 0)
+    relay(0, z >= n // 2)
 
     for way, has in ((0, z > 0), (1, z < n - 1)):
         @pl.when(has)
@@ -289,7 +300,7 @@
     experts = capacity.shape[0]
     slot_count = -(-(3 * tok_rows // experts) // 8) * 8
     head_out = exchange_experts(
-        n_seq, n_sub, slot_count, sub_tok, expert_ids[0].T, combine_q[0].T, capacity[:, None],
+        n_seq, n_sub, slot_count, sub_tok, expert_ids[0].T, combine_q[0].T, capacity[None, :],
         expert_in[0], expert_out[0])
     return merge_scatter(n_sub, head_out, w_merge)
 

time: 133 us -> 127 us (0.955)
  the two profiles are of different devices: /device:TPU:14 before, /device:TPU:0 now
where the time goes in v3:
time: 127 us; the launch traced here: 126 us
  Pallas kernels  118 us (93%)
  matrix products  5.86 us (5%)
  local copies, waits for them, and re-layouts  2.41 us (2%)
    pallas_call x1, Pallas kernels, exchange_experts(): pl.pallas_call(functools.partial(experts_kernel, n_seq, n_sub, slots), ou...  81.9 us
    pallas_call x1, Pallas kernels, merge_scatter(): pl.pallas_call(functools.partial(merge_kernel, n), out_shape=jax.ShapeDty...  36.1 us
    dot_general x1, matrix products, body(): jnp.dot(tokens, w_split, preferred_element_type=jnp.float32)  5.86 us

profile of v3, /device:TPU:0, one launch (start us, length us, event | category | flops | bytes accessed | tf_op | source)
XLA Modules:
  0.0 126.4 jit_solution(1604765754997439813)
XLA Ops:
  0.0 0.0 copy-start
  0.0 1.6 %copy-done = bf16[256,4096]{1,0:T(8,128)(2,1)S(1)} copy-done((bf16[256,4096]{1,0:T(8,128)(2,1)S(1)}, bf16[256,4096]{1,0:T(8,128)(2,1)}, u32[]{:S(2)}) %copy-start) | copy-done | bytes 2097176
  1.6 0.0 copy-start.2
  1.6 0.0 copy-start.3
  1.6 0.0 copy-start.4
  1.6 0.0 copy-start.5
  1.6 0.0 copy-start.6
  1.6 0.0 copy-start.1
  1.6 5.9 %convolution_convert_fusion.sub_tok = bf16[256,1024]{1,0:T(8,128)(2,1)S(1)} fusion(bf16[256,4096]{1,0:T(8,128)(2,1)S(1)} %copy-done, bf16[4096,1024]{1,0:T(8,128)(2,1)} %param.9), kind=kOutput, calls=%fused_computation | convolution fusion | flops 2147745792 | bytes 11010048 | tf_op jit(solution)/shard_map/dot_general | solution.py:297
  7.5 0.0 copy-done.2
  7.5 0.0 copy-done.3
  7.5 0.0 copy-done.4
  7.5 0.0 copy-done.5
  7.5 0.0 copy-done.6
  7.5 81.9 %experts.1.head = bf16[256,1024]{1,0:T(8,128)(2,1)S(1)} custom-call(bf16[256,1024]{1,0:T(8,128)(2,1)S(1)} %convolution_convert_fusion.sub_tok, s32[2,256]{1,0:T(2,128)S(1)} %bitcast.13, s32[2,256]{1,0:T(2,128)S(1)} %bitcast.14, s32[1,32]{1,0:T(1,128)S(1)} %bitcast.15, bf16[1024,2048]{1,0:T(8,128)(2,1)S(1)} %bitcast.11, bf16[1024,1024]{1,0:T(8,128)(2,1)S(1)} %bitcast.12), custom_call_target="tpu_custom_call" | custom-call | tf_op jit(solution)/shard_map/experts/pallas_call | solution.py:167
  89.5 0.0 copy-done.1
  89.5 36.1 %merge.1 = bf16[256,1024]{1,0:T(8,128)(2,1)S(1)} custom-call(bf16[256,1024]{1,0:T(8,128)(2,1)S(1)} %experts.1.head, bf16[1024,4096]{1,0:T(8,128)(2,1)S(1)} %copy-done.1), custom_call_target="tpu_custom_call" | custom-call | tf_op jit(solution)/shard_map/merge/pallas_call | solution.py:277
  125.6 0.8 copy.10
Async XLA Ops:
  0.0 1.6 %copy-start = (bf16[256,4096]{1,0:T(8,128)(2,1)S(1)}, bf16[256,4096]{1,0:T(8,128)(2,1)}, u32[]{:S(2)}) copy-start(bf16[256,4096]{1,0:T(8,128)(2,1)} %param.8) | copy-start | bytes 6291460
  1.6 5.9 %copy-start.2 = (bf16[1,1024,2048]{2,1,0:T(8,128)(2,1)S(1)}, bf16[1,1024,2048]{2,1,0:T(8,128)(2,1)}, u32[]{:S(2)}) copy-start(bf16[1,1024,2048]{2,1,0:T(8,128)(2,1)} %param.11) | copy-start | bytes 12582916
  1.6 5.9 %copy-start.3 = (bf16[1,1024,1024]{2,1,0:T(8,128)(2,1)S(1)}, bf16[1,1024,1024]{2,1,0:T(8,128)(2,1)}, u32[]{:S(2)}) copy-start(bf16[1,1024,1024]{2,1,0:T(8,128)(2,1)} %param.12) | copy-start | bytes 6291460
  1.6 5.9 %copy-start.4 = (s32[1,256,2]{1,2,0:T(2,128)S(1)}, s32[1,256,2]{1,2,0:T(2,128)}, u32[]{:S(2)}) copy-start(s32[1,256,2]{1,2,0:T(2,128)} %param.13) | copy-start | bytes 6148
  1.6 5.9 %copy-start.5 = (s32[1,256,2]{1,2,0:T(2,128)S(1)}, s32[1,256,2]{1,2,0:T(2,128)}, u32[]{:S(2)}) copy-start(s32[1,256,2]{1,2,0:T(2,128)} %param.14) | copy-start | bytes 6148
  1.6 5.9 %copy-start.6 = (s32[32]{0:T(128)S(1)}, s32[32]{0:T(128)}, u32[]{:S(2)}) copy-start(s32[32]{0:T(128)} %param.15) | copy-start | bytes 388
  1.6 87.9 %copy-start.1 = (bf16[1024,4096]{1,0:T(8,128)(2,1)S(1)}, bf16[1024,4096]{1,0:T(8,128)(2,1)}, u32[]{:S(2)}) copy-start(bf16[1024,4096]{1,0:T(8,128)(2,1)} %w) | copy-start | bytes 25165828
